TPU v7x, 32 devices: a whole 2x2x4 slice. The times are simulated.
32 devices in a mesh: patch: 16 (over z, y, x), batch: 2 (over core).
Axes of the slice: x: 2, y: 2, z: 4, core: 2. Of those that a mesh axis runs over, the one named last changes fastest.
Arguments:
- tokens: bfloat16 [4096, 1152], P(('batch', 'patch')), parts along dimension 0, may hold values from -6 to 6
- slots: int32 [4096], P(('batch', 'patch')), parts along dimension 0, may hold values from 0 to 127, as said below
- counts: int32 [32], P(('batch', 'patch')), parts along dimension 0, may hold values from 32 to 128, as said below
- shift: float32 [1152], replicated, may hold values from -3 to 3
- scale: float32 [1152], replicated, may hold values from -3 to 3
- gate: float32 [1152], replicated, may hold values from -4 to 4
- w_qkv: bfloat16 [1152, 3456], replicated, may hold values from -1 to 1
- w_out: bfloat16 [1152, 1152], replicated, may hold values from -0.1875 to 0.1875
Outputs:
- result: bfloat16 [4096, 1152], P(('batch', 'patch')), parts along dimension 0
There are 2 independent parts, one for each index of `batch`. A program takes and returns all parts, laid end to end along the dimension named above; an argument that names none is the same for every part. Nothing has to cross between parts.
Inputs may be any that keep to these rules, and one draw needn't show every extreme that they name: `counts`: at least a quarter of each block's slots are live. The live slots of all blocks of an image number exactly 80 times the number of patch devices, and all blocks of some device are full. `slots`: every token's slot is below its block's count, and every slot below the count holds at least one token.
All inputs are finite; a program needn't handle non-finite values.
Results may differ from a plain program's by a relative error of at most 0.011.
Values may be sent and summed in bfloat16 or wider, within the bound.
A program may use at most 192 MiB of HBM per device.

v0:
```python
import jax
import jax.numpy as jnp
from jax import lax
from jax.sharding import PartitionSpec as P

HEADS = 16
BLK = 128


def layer_norm(merged, shift, scale):
    values = merged.astype(jnp.float32)
    center = jnp.mean(values, axis=-1, keepdims=True)
    spread = jnp.mean((values - center) ** 2, axis=-1, keepdims=True)
    return ((values - center) * lax.rsqrt(spread + 1e-06) * (1.0 + scale) + shift).astype(
        jnp.bfloat16
    )


def size_bias(sizes):
    return jnp.log(jnp.maximum(sizes.astype(jnp.float32), 1.0))


def empty_carry(heads, query_rows, head_size):
    return (
        jnp.full((heads, query_rows), -1e30, jnp.float32),
        jnp.zeros((heads, query_rows), jnp.float32),
        jnp.zeros((heads, query_rows, head_size), jnp.float32),
    )


def finish(accum, total):
    heads, query_rows, head_size = accum.shape
    return (
        (accum / total[:, :, None])
        .transpose(1, 0, 2)
        .reshape(query_rows, heads * head_size)
        .astype(jnp.bfloat16)
    )


def attend_piece(query, carry, keys, values, bias, inverse):
    top, total, accum = carry
    key_rows = keys.shape[0]
    heads = query.shape[1]
    key_heads = keys.reshape(key_rows, heads, -1)
    value_heads = values.reshape(key_rows, heads, -1)
    score = (
        jnp.einsum("qhe,khe->hqk", query, key_heads, preferred_element_type=jnp.float32) * inverse
        + bias[None, None, :]
    )
    new_top = jnp.maximum(top, jnp.max(score, axis=-1))
    probs = jnp.exp(score - new_top[:, :, None])
    total = jnp.sum(probs, axis=-1)
    update = jnp.einsum(
        "hqk,khe->hqe", probs.astype(jnp.bfloat16), value_heads, preferred_element_type=jnp.float32
    )
    return (new_top, total, update)


def body(tokens, slots, counts, shift, scale, gate, w_qkv, w_out):
    rows, width = tokens.shape
    nblk = rows // BLK
    heads = HEADS
    head_size = width // heads
    inverse = 1.0 / head_size**0.5
    onehot = slots.reshape(nblk, BLK)[:, :, None] == jnp.arange(BLK, dtype=jnp.int32)[None, None, :]
    sums = jnp.einsum(
        "bts,btd->bsd",
        onehot.astype(jnp.bfloat16),
        tokens.reshape(nblk, BLK, width),
        preferred_element_type=jnp.float32,
    )
    members = jnp.sum(onehot.astype(jnp.float32), axis=1)
    merged = (
        (sums / jnp.maximum(members, 1.0)[:, :, None]).astype(jnp.bfloat16).reshape(rows, width)
    )
    normed = layer_norm(merged, shift, scale)
    sizes = members.reshape(rows).astype(jnp.bfloat16)
    qkv = jnp.dot(normed, w_qkv, preferred_element_type=jnp.float32)
    query = qkv[:, :width].astype(jnp.bfloat16)
    keys = qkv[:, width : 2 * width].astype(jnp.bfloat16)
    values = qkv[:, 2 * width :].astype(jnp.bfloat16)
    alive = (
        (jnp.arange(BLK, dtype=jnp.int32)[None, :] < counts[:, None])
        .reshape(rows)
        .astype(jnp.bfloat16)
    )
    query_heads = query.reshape(rows, heads, head_size)
    keys_part = lax.all_gather(keys, "patch", axis=0, tiled=True)
    values_part = lax.all_gather(values, "patch", axis=0, tiled=True)
    sizes_part = lax.all_gather(sizes, "patch", axis=0, tiled=True)
    alive_part = lax.all_gather(alive, "patch", axis=0, tiled=True)
    bias = jnp.where(alive_part > 0, size_bias(sizes_part), -1e30)
    top, total, accum = attend_piece(
        query_heads, empty_carry(heads, rows, head_size), keys_part, values_part, bias, inverse
    )
    attended = finish(accum, total)
    projected = jnp.dot(attended, w_out, preferred_element_type=jnp.float32)
    branch = jnp.einsum(
        "bts,bsd->btd",
        onehot.astype(jnp.float32),
        projected.reshape(nblk, BLK, width),
        precision=lax.Precision.HIGHEST,
    ).reshape(rows, width)
    return (tokens.astype(jnp.float32) + gate * branch).astype(jnp.bfloat16)


def solution(mesh):
    return jax.shard_map(
        body,
        mesh=mesh,
        in_specs=(
            P(("batch", "patch"), None),
            P(("batch", "patch")),
            P(("batch", "patch")),
            P(),
            P(),
            P(),
            P(),
            P(),
        ),
        out_specs=P(("batch", "patch"), None),
        check_vma=False,
    )
```

profile of v0, /device:TPU:0, one launch (start us, length us, event | category | flops | bytes accessed | tf_op | source)
XLA Modules:
  0.0 205.7 jit_solution(10820672473933980348)
XLA Ops:
  6.5 0.0 copy-start
  6.5 0.0 all-gather.5.cloned.1.call-start
  6.5 0.9 convert_reduce_fusion
  7.5 1.4 fusion.27
  8.9 0.2 multiply_reduce_fusion
  9.1 0.7 broadcast_add_fusion
  9.8 4.7 %convolution_convert_fusion = bf16[128,3456]{1,0:T(8,128)(2,1)S(1)} fusion(bf16[1152,3456]{1,0:T(8,128)(2,1)} %param.14, f32[128,1152]{1,0:T(8,128)S(1)} %get-tuple-element.11, f32[1152]{0:T(1024)} %param.11, f32[1152]{0:T(1024)S(1)} %broadcast_add_fusion, f32[128]{0:T(128)S(1)} %add_rsqrt_fusion, f32[128]{0:T(128)S(1)} %broadcast_multiply_fusion), kind=kOutput, calls=%fused_computation.6 | convolution fusion | flops 1020395520 | bytes 9447424 | tf_op jit(solution)/shard_map/dot_general | solution.py:79
  14.5 0.9 fusion.26
  15.4 0.0 all-gather.5.cloned.1.call-update
  15.4 0.0 all-gather.7.cloned.1.call-start
  15.5 0.7 all-gather.7.cloned.1.call-update
  16.2 0.2 copy.18
  17.1 42.7 %all-gather.1 = bf16[16,1,128]{2,1,0:T(2,128)(2,1)S(1)} all-gather(bf16[1,1,128]{2,1,0:T(2,128)(2,1)S(1)} %get-tuple-element.8), channel_id=1, replica_groups=mesh['patch'=16,'batch'=2] {'patch'}, dimensions={0}, use_global_device_ids=true | all-gather | bytes 4352 | tf_op jit(solution)/shard_map/all_gather | solution.py:91
  59.7 36.4 %all-gather = bf16[16,1,128]{2,1,0:T(2,128)(2,1)S(1)} all-gather(bf16[1,1,128]{2,1,0:T(2,128)(2,1)S(1)} %fusion.24), channel_id=1, replica_groups=mesh['patch'=16,'batch'=2] {'patch'}, dimensions={0}, use_global_device_ids=true | all-gather | bytes 4352 | tf_op jit(solution)/shard_map/all_gather | solution.py:92
  96.1 2.0 all-gather.5.cloned.1.call-done
  98.1 6.7 %copy.19 = bf16[2048,1152]{0,1:T(8,128)(2,1)} copy(bf16[2048,1152]{1,0:T(8,128)(2,1)} %all-gather.5.cloned.1.call-done) | data formatting | bytes 9437184 | tf_op jit(solution)/shard_map/all_gather | solution.py:89
  104.9 4.5 %fusion = (f32[16,128]{1,0:T(8,128)S(1)}, f32[16,128,2048]{2,1,0:T(8,128)S(1)}) fusion(f32[2048]{0:T(1024)S(1)} %bitcast.30, bf16[128,16,72]{0,2,1:T(8,128)(2,1)S(1)} %bitcast.28, bf16[2048,16,72]{0,2,1:T(8,128)(2,1)} %bitcast.26), kind=kOutput, calls=%fused_computation.2 | convolution fusion | flops 616560640 | bytes 21807104 | tf_op jit(solution)/shard_map/qhe,khe->hqk/dot_general | solution.py:48
  109.3 0.0 copy-start.1
  109.4 5.7 %copy-done.1 = f32[16,128,2048]{2,1,0:T(8,128)} copy-done((f32[16,128,2048]{2,1,0:T(8,128)}, f32[16,128,2048]{2,1,0:T(8,128)S(1)}, u32[]{:S(2)}) %copy-start.1) | copy-done | bytes 16777240
  115.1 3.8 %fusion.1 = f32[16,128]{1,0:T(8,128)S(1)} fusion(f32[16,128,2048]{2,1,0:T(8,128)S(1)} %get-tuple-element.13, f32[16,128]{1,0:T(8,128)S(1)} %broadcast_maximum_fusion, f32[2048]{0:T(1024)S(1)} %bitcast.31), kind=kLoop, calls=%fused_computation.3 | loop fusion | flops 16775168 | bytes 16801792 | tf_op jit(solution)/shard_map/reduce_sum | solution.py:53
  118.8 60.6 %all-gather.7.cloned.1.call-done = bf16[2048,1152]{1,0:T(8,128)(2,1)} async-done(((bf16[128,1152]{1,0:T(8,128)(2,1)}), bf16[2048,1152]{1,0:T(8,128)(2,1)}) %all-gather.7.cloned.1.call-update) | async-done | bytes 4718608 | tf_op jit(solution)/shard_map/all_gather | solution.py:90
  179.4 6.7 %copy.20 = bf16[2048,1152]{0,1:T(8,128)(2,1)} copy(bf16[2048,1152]{1,0:T(8,128)(2,1)} %all-gather.7.cloned.1.call-done) | data formatting | bytes 9437184 | tf_op jit(solution)/shard_map/all_gather | solution.py:90
  186.1 0.0 copy-start.2
  186.1 0.0 copy-start.3
  186.1 0.0 copy-start.4
  186.1 10.9 %fusion.15 = bf16[128,16,72]{0,2,1:T(8,128)(2,1)S(1)} fusion(bf16[2048,16,72]{0,2,1:T(8,128)(2,1)} %bitcast.27, f32[16,128,2048]{2,1,0:T(8,128)} %copy-done.1, f32[16,128]{1,0:T(8,128)S(1)} %broadcast_maximum_fusion, f32[2048]{0:T(1024)S(1)} %bitcast.32, f32[128,16]{0,1:T(8,128)S(1)} %bitcast.33), kind=kOutput, calls=%fused_computation.15 | convolution fusion | flops 621051904 | bytes 21815296 | tf_op jit(solution)/shard_map/hqk,khe->hqe/dot_general | solution.py:54
  197.0 0.0 copy-done
  197.0 0.6 fusion.28
  197.6 0.0 copy-done.2
  197.6 0.0 copy-done.3
  197.7 0.0 copy-done.4
  197.7 1.2 fusion.8
  (6 shorter events, 0.1 us)
Async XLA Ops:
  6.5 190.5 %copy-start = (bf16[1152,1152]{1,0:T(8,128)(2,1)S(1)}, bf16[1152,1152]{1,0:T(8,128)(2,1)}, u32[]{:S(2)}) copy-start(bf16[1152,1152]{1,0:T(8,128)(2,1)} %param.15) | copy-start | bytes 7962628
  6.5 91.6 %all-gather.5.cloned.1.call-start = ((), (), s32[]{:S(2)}) async-start(), calls=%async_computation | async-start | bytes 5013504 | tf_op jit(solution)/shard_map/all_gather | solution.py:89
  15.4 163.9 %all-gather.7.cloned.1.call-start = ((), (), s32[]{:S(2)}) async-start(), calls=%async_computation.1 | async-start | bytes 5013504 | tf_op jit(solution)/shard_map/all_gather | solution.py:90
  109.3 5.7 %copy-start.1 = (f32[16,128,2048]{2,1,0:T(8,128)}, f32[16,128,2048]{2,1,0:T(8,128)S(1)}, u32[]{:S(2)}) copy-start(f32[16,128,2048]{2,1,0:T(8,128)S(1)} %get-tuple-element.13) | copy-start | bytes 50331652
  186.1 11.5 %copy-start.2 = (bf16[128,1152]{1,0:T(8,128)(2,1)S(1)}, bf16[128,1152]{1,0:T(8,128)(2,1)}, u32[]{:S(2)}) copy-start(bf16[128,1152]{1,0:T(8,128)(2,1)} %param.8) | copy-start | bytes 884740
  186.1 11.5 %copy-start.3 = (f32[1152]{0:T(1024)S(1)}, f32[1152]{0:T(1024)}, u32[]{:S(2)}) copy-start(f32[1152]{0:T(1024)} %param.13) | copy-start | bytes 13828
  186.1 11.5 %copy-start.4 = (s32[128]{0:T(128)S(1)}, s32[128]{0:T(128)}, u32[]{:S(2)}) copy-start(s32[128]{0:T(128)} %param.9) | copy-start | bytes 1540
Sparse Core Ops, SparseCore 0:
  15.6 82.5 all-gather.4
  100.9 78.4 all-gather.6
where the time goes:
time: 206 us
  blocking collectives  79 us (38%)
  waiting for transfers between devices  63.3 us (31%)
  matrix products  23.3 us (11%)
  local copies, waits for them, and re-layouts  20.3 us (10%)
  between operations  14.2 us (7%)
  other arithmetic  5.63 us (3%)
    all_gather x1, waiting for transfers between devices, body(): values_part = lax.all_gather(values, 'patch', axis=0, tiled=True)  60.6 us
    all_gather x1, blocking collectives, body(): sizes_part = lax.all_gather(sizes, 'patch', axis=0, tiled=True)  42.7 us
    all_gather x1, blocking collectives, body(): alive_part = lax.all_gather(alive, 'patch', axis=0, tiled=True)  36.4 us
    dot_general x1, matrix products, attend_piece(): jnp.einsum('hqk,khe->hqe', probs.astype(jnp.bfloat16), value_heads, prefe...  10.9 us
    all_gather x1, local copies, waits for them, and re-layouts, body(): values_part = lax.all_gather(values, 'patch', axis=0, tiled=True)  6.74 us
    all_gather x1, local copies, waits for them, and re-layouts, body(): keys_part = lax.all_gather(keys, 'patch', axis=0, tiled=True)  6.74 us
    unnamed x10, local copies, waits for them, and re-layouts  5.71 us
    dot_general x1, matrix products, body(): qkv = jnp.dot(normed, w_qkv, preferred_element_type=jnp.float32)  4.71 us
  transfers between devices with their start and end apart: 2, of which 2 were waited for; matrix products, arithmetic and copies ran while one was open for 7% of the time, Pallas kernels for 0%

commit v1 on v0

--- a/solution.py
+++ b/solution.py
@@ -87,7 +87,13 @@
     )
     query_heads = query.reshape(rows, heads, head_size)
     keys_part = lax.all_gather(keys, "patch", axis=0, tiled=True)
-    values_part = lax.all_gather(values, "patch", axis=0, tiled=True)
+    size = lax.axis_size("patch")
+    held, pieces = (values, [values])
+    for _ in range(size - 1):
+        held = lax.ppermute(held, "patch", [(i, (i + 1) % size) for i in range(size)])
+        pieces.insert(0, held)
+    flat = jnp.concatenate(pieces, axis=0)
+    values_part = jnp.roll(flat, (lax.axis_index("patch") + 1) * values.shape[0], axis=0)
     sizes_part = lax.all_gather(sizes, "patch", axis=0, tiled=True)
     alive_part = lax.all_gather(alive, "patch", axis=0, tiled=True)
     bias = jnp.where(alive_part > 0, size_bias(sizes_part), -1e30)

time: 206 us -> 319 us (1.55)
  waiting for transfers between devices: 63.3 us -> 168 us
  local copies, waits for them, and re-layouts: 20.3 us -> 29.7 us
  blocking collectives: 79 us -> 74.6 us
    ppermute x0 -> x15, waiting for transfers between devices: none -> 168 us  [body(): lax.ppermute(held, 'patch', [(i, (i + 1) % size) for i in range(size)])]
    all_gather x1 -> x0, waiting for transfers between devices: 60.6 us -> none  [body(): values_part = lax.all_gather(values, 'patch', axis=0, tiled=True)]
    dynamic_slice x0 -> x2, local copies, waits for them, and re-layouts: none -> 11.6 us  [body(): jnp.roll(flat, (lax.axis_index('patch') + 1) * values.shape[0], axis=0)]
    all_gather x1, blocking collectives: 42.7 us -> 35.6 us  [body(): sizes_part = lax.all_gather(sizes, 'patch', axis=0, tiled=True)]
    all_gather x1 -> x0, local copies, waits for them, and re-layouts: 6.74 us -> none  [body(): values_part = lax.all_gather(values, 'patch', axis=0, tiled=True)]
    unnamed x10 -> x43, local copies, waits for them, and re-layouts: 5.71 us -> 10.4 us
  transfers between devices with their start and end apart: 2 -> 16, of which waited for: 2 -> 15; matrix products, arithmetic and copies ran while one was open for 7% -> 4% of each run, Pallas kernels for 0% -> 0%
where the time goes in v1:
time: 319 us
  waiting for transfers between devices  168 us (53%)
  blocking collectives  74.6 us (23%)
  local copies, waits for them, and re-layouts  29.7 us (9%)
  matrix products  23.3 us (7%)
  between operations  14.4 us (5%)
  other arithmetic  5.62 us (2%)
    ppermute x15, waiting for transfers between devices, body(): lax.ppermute(held, 'patch', [(i, (i + 1) % size) for i in range(size)])  168 us
    all_gather x1, blocking collectives, body(): alive_part = lax.all_gather(alive, 'patch', axis=0, tiled=True)  39.1 us
    all_gather x1, blocking collectives, body(): sizes_part = lax.all_gather(sizes, 'patch', axis=0, tiled=True)  35.6 us
    dynamic_slice x2, local copies, waits for them, and re-layouts, body(): jnp.roll(flat, (lax.axis_index('patch') + 1) * values.shape[0], axis=0)  11.6 us
    dot_general x1, matrix products, attend_piece(): jnp.einsum('hqk,khe->hqe', probs.astype(jnp.bfloat16), value_heads, prefe...  10.8 us
    unnamed x43, local copies, waits for them, and re-layouts  10.4 us
    all_gather x1, local copies, waits for them, and re-layouts, body(): keys_part = lax.all_gather(keys, 'patch', axis=0, tiled=True)  6.74 us
  transfers between devices with their start and end apart: 16, of which 15 were waited for; matrix products, arithmetic and copies ran while one was open for 4% of the time, Pallas kernels for 0%

profile of v1, /device:TPU:0, one launch (start us, length us, event | category | flops | bytes accessed | tf_op | source)
XLA Modules:
  0.0 318.6 jit_solution(2972510719511307166)
XLA Ops:
  6.5 0.9 convert_reduce_fusion
  7.5 0.7 broadcast_add_fusion
  8.2 1.4 fusion.27
  9.6 0.2 multiply_reduce_fusion
  9.8 4.7 %convolution_convert_fusion = bf16[128,3456]{1,0:T(8,128)(2,1)S(1)} fusion(bf16[1152,3456]{1,0:T(8,128)(2,1)} %param.14, f32[128,1152]{1,0:T(8,128)S(1)} %get-tuple-element.11, f32[1152]{0:T(1024)} %param.11, f32[1152]{0:T(1024)S(1)} %broadcast_add_fusion, f32[128]{0:T(128)S(1)} %add_rsqrt_fusion, f32[128]{0:T(128)S(1)} %broadcast_multiply_fusion), kind=kOutput, calls=%fused_computation.6 | convolution fusion | flops 1020395520 | bytes 9447424 | tf_op jit(solution)/shard_map/dot_general | solution.py:79
  14.6 3.0 collective-permute-start
  17.6 11.0 %collective-permute-done = bf16[128,1152]{1,0:T(8,128)(2,1)S(1)} collective-permute-done((bf16[128,1152]{1,0:T(8,128)(2,1)S(1)}, bf16[128,1152]{1,0:T(8,128)(2,1)S(1)}, u32[]{:S(2)}, u32[]{:S(2)}) %collective-permute-start) | collective-permute-done | bytes 294944 | tf_op jit(solution)/shard_map/ppermute | solution.py:93
  28.6 0.0 collective-permute-start.1
  28.6 11.8 %collective-permute-done.1 = bf16[128,1152]{1,0:T(8,128)(2,1)S(1)} collective-permute-done((bf16[128,1152]{1,0:T(8,128)(2,1)S(1)}, bf16[128,1152]{1,0:T(8,128)(2,1)S(1)}, u32[]{:S(2)}, u32[]{:S(2)}) %collective-permute-start.1) | collective-permute-done | bytes 294944 | tf_op jit(solution)/shard_map/ppermute | solution.py:93
  40.4 0.0 collective-permute-start.2
  40.4 10.9 %collective-permute-done.2 = bf16[128,1152]{1,0:T(8,128)(2,1)S(1)} collective-permute-done((bf16[128,1152]{1,0:T(8,128)(2,1)S(1)}, bf16[128,1152]{1,0:T(8,128)(2,1)S(1)}, u32[]{:S(2)}, u32[]{:S(2)}) %collective-permute-start.2) | collective-permute-done | bytes 294944 | tf_op jit(solution)/shard_map/ppermute | solution.py:93
  51.3 0.0 collective-permute-start.3
  51.3 10.3 %collective-permute-done.3 = bf16[128,1152]{1,0:T(8,128)(2,1)S(1)} collective-permute-done((bf16[128,1152]{1,0:T(8,128)(2,1)S(1)}, bf16[128,1152]{1,0:T(8,128)(2,1)S(1)}, u32[]{:S(2)}, u32[]{:S(2)}) %collective-permute-start.3) | collective-permute-done | bytes 294944 | tf_op jit(solution)/shard_map/ppermute | solution.py:93
  61.6 0.0 collective-permute-start.4
  61.6 10.3 %collective-permute-done.4 = bf16[128,1152]{1,0:T(8,128)(2,1)S(1)} collective-permute-done((bf16[128,1152]{1,0:T(8,128)(2,1)S(1)}, bf16[128,1152]{1,0:T(8,128)(2,1)S(1)}, u32[]{:S(2)}, u32[]{:S(2)}) %collective-permute-start.4) | collective-permute-done | bytes 294944 | tf_op jit(solution)/shard_map/ppermute | solution.py:93
  71.9 0.0 collective-permute-start.5
  71.9 10.3 %collective-permute-done.5 = bf16[128,1152]{1,0:T(8,128)(2,1)S(1)} collective-permute-done((bf16[128,1152]{1,0:T(8,128)(2,1)S(1)}, bf16[128,1152]{1,0:T(8,128)(2,1)S(1)}, u32[]{:S(2)}, u32[]{:S(2)}) %collective-permute-start.5) | collective-permute-done | bytes 294944 | tf_op jit(solution)/shard_map/ppermute | solution.py:93
  82.2 0.0 collective-permute-start.6
  82.2 11.2 %collective-permute-done.6 = bf16[128,1152]{1,0:T(8,128)(2,1)S(1)} collective-permute-done((bf16[128,1152]{1,0:T(8,128)(2,1)S(1)}, bf16[128,1152]{1,0:T(8,128)(2,1)S(1)}, u32[]{:S(2)}, u32[]{:S(2)}) %collective-permute-start.6) | collective-permute-done | bytes 294944 | tf_op jit(solution)/shard_map/ppermute | solution.py:93
  93.4 0.0 collective-permute-start.7
  93.4 12.3 %collective-permute-done.7 = bf16[128,1152]{1,0:T(8,128)(2,1)S(1)} collective-permute-done((bf16[128,1152]{1,0:T(8,128)(2,1)S(1)}, bf16[128,1152]{1,0:T(8,128)(2,1)S(1)}, u32[]{:S(2)}, u32[]{:S(2)}) %collective-permute-start.7) | collective-permute-done | bytes 294944 | tf_op jit(solution)/shard_map/ppermute | solution.py:93
  105.7 13.5 %collective-permute-done.8 = bf16[128,1152]{1,0:T(8,128)(2,1)S(1)} collective-permute-done((bf16[128,1152]{1,0:T(8,128)(2,1)S(1)}, bf16[128,1152]{1,0:T(8,128)(2,1)S(1)}, u32[]{:S(2)}, u32[]{:S(2)}) %collective-permute-start.8) | collective-permute-done | bytes 294944 | tf_op jit(solution)/shard_map/ppermute | solution.py:93
  119.2 12.6 %collective-permute-done.9 = bf16[128,1152]{1,0:T(8,128)(2,1)S(1)} collective-permute-done((bf16[128,1152]{1,0:T(8,128)(2,1)S(1)}, bf16[128,1152]{1,0:T(8,128)(2,1)S(1)}, u32[]{:S(2)}, u32[]{:S(2)}) %collective-permute-start.9) | collective-permute-done | bytes 294944 | tf_op jit(solution)/shard_map/ppermute | solution.py:93
  131.8 0.0 collective-permute-start.10
  131.8 11.8 %collective-permute-done.10 = bf16[128,1152]{1,0:T(8,128)(2,1)S(1)} collective-permute-done((bf16[128,1152]{1,0:T(8,128)(2,1)S(1)}, bf16[128,1152]{1,0:T(8,128)(2,1)S(1)}, u32[]{:S(2)}, u32[]{:S(2)}) %collective-permute-start.10) | collective-permute-done | bytes 294944 | tf_op jit(solution)/shard_map/ppermute | solution.py:93
  143.6 10.9 %collective-permute-done.11 = bf16[128,1152]{1,0:T(8,128)(2,1)S(1)} collective-permute-done((bf16[128,1152]{1,0:T(8,128)(2,1)S(1)}, bf16[128,1152]{1,0:T(8,128)(2,1)S(1)}, u32[]{:S(2)}, u32[]{:S(2)}) %collective-permute-start.11) | collective-permute-done | bytes 294944 | tf_op jit(solution)/shard_map/ppermute | solution.py:93
  154.5 10.3 %collective-permute-done.12 = bf16[128,1152]{1,0:T(8,128)(2,1)S(1)} collective-permute-done((bf16[128,1152]{1,0:T(8,128)(2,1)S(1)}, bf16[128,1152]{1,0:T(8,128)(2,1)S(1)}, u32[]{:S(2)}, u32[]{:S(2)}) %collective-permute-start.12) | collective-permute-done | bytes 294944 | tf_op jit(solution)/shard_map/ppermute | solution.py:93
  164.8 0.0 collective-permute-start.13
  164.8 10.3 %collective-permute-done.13 = bf16[128,1152]{1,0:T(8,128)(2,1)S(1)} collective-permute-done((bf16[128,1152]{1,0:T(8,128)(2,1)S(1)}, bf16[128,1152]{1,0:T(8,128)(2,1)S(1)}, u32[]{:S(2)}, u32[]{:S(2)}) %collective-permute-start.13) | collective-permute-done | bytes 294944 | tf_op jit(solution)/shard_map/ppermute | solution.py:93
  175.2 10.3 %collective-permute-done.14 = bf16[128,1152]{1,0:T(8,128)(2,1)S(1)} collective-permute-done((bf16[128,1152]{1,0:T(8,128)(2,1)S(1)}, bf16[128,1152]{1,0:T(8,128)(2,1)S(1)}, u32[]{:S(2)}, u32[]{:S(2)}) %collective-permute-start.14) | collective-permute-done | bytes 294944 | tf_op jit(solution)/shard_map/ppermute | solution.py:93
  186.7 0.8 fusion.26
  187.5 3.6 %copy-done.2 = bf16[4096,1152]{1,0:T(8,128)(2,1)} copy-done((bf16[4096,1152]{1,0:T(8,128)(2,1)}, bf16[4096,1152]{1,0:T(8,128)(2,1)S(1)}, u32[]{:S(2)}) %copy-start.2) | copy-done | bytes 9437208
  191.1 0.0 all-gather.4.cloned.1.call-update
  191.8 35.6 %all-gather.1 = bf16[16,1,128]{2,1,0:T(2,128)(2,1)S(1)} all-gather(bf16[1,1,128]{2,1,0:T(2,128)(2,1)S(1)} %get-tuple-element.8), channel_id=1, replica_groups=mesh['patch'=16,'batch'=2] {'patch'}, dimensions={0}, use_global_device_ids=true | all-gather | bytes 4352 | tf_op jit(solution)/shard_map/all_gather | solution.py:97
  227.4 39.1 %all-gather = bf16[16,1,128]{2,1,0:T(2,128)(2,1)S(1)} all-gather(bf16[1,1,128]{2,1,0:T(2,128)(2,1)S(1)} %fusion.24), channel_id=1, replica_groups=mesh['patch'=16,'batch'=2] {'patch'}, dimensions={0}, use_global_device_ids=true | all-gather | bytes 4352 | tf_op jit(solution)/shard_map/all_gather | solution.py:98
  266.5 0.2 copy.17
  266.7 4.9 %constant_dynamic-slice_fusion = bf16[2048,1152]{1,0:T(8,128)(2,1)} fusion(bf16[4096,1152]{1,0:T(8,128)(2,1)} %copy-done.2, s32[]{:T(128)S(6)} %select_n.19), kind=kLoop, calls=%fused_computation.66 | loop fusion | bytes 9437188 | tf_op jit(solution)/shard_map/jit(_roll_dynamic)/dynamic_slice | solution.py:96
  271.6 6.7 %copy.19 = bf16[2048,1152]{0,1:T(8,128)(2,1)} copy(bf16[2048,1152]{1,0:T(8,128)(2,1)} %constant_dynamic-slice_fusion) | data formatting | bytes 9437184 | tf_op jit(solution)/shard_map/jit(_roll_dynamic)/dynamic_slice | solution.py:96
  278.3 6.7 %copy.18 = bf16[2048,1152]{0,1:T(8,128)(2,1)} copy(bf16[2048,1152]{1,0:T(8,128)(2,1)} %all-gather.4.cloned.1.call-done) | data formatting | bytes 9437184 | tf_op jit(solution)/shard_map/all_gather | solution.py:89
  285.0 4.5 %fusion = (f32[16,128]{1,0:T(8,128)S(1)}, f32[16,128,2048]{2,1,0:T(8,128)S(1)}) fusion(f32[2048]{0:T(1024)S(1)} %bitcast.30, bf16[128,16,72]{0,2,1:T(8,128)(2,1)S(1)} %bitcast.28, bf16[2048,16,72]{0,2,1:T(8,128)(2,1)} %bitcast.26), kind=kOutput, calls=%fused_computation.2 | convolution fusion | flops 616560640 | bytes 21807104 | tf_op jit(solution)/shard_map/qhe,khe->hqk/dot_general | solution.py:48
  289.6 5.7 %copy-done.1 = f32[16,128,2048]{2,1,0:T(8,128)} copy-done((f32[16,128,2048]{2,1,0:T(8,128)}, f32[16,128,2048]{2,1,0:T(8,128)S(1)}, u32[]{:S(2)}) %copy-start.1) | copy-done | bytes 16777240
  295.3 3.8 %fusion.1 = f32[16,128]{1,0:T(8,128)S(1)} fusion(f32[16,128,2048]{2,1,0:T(8,128)S(1)} %get-tuple-element.13, f32[16,128]{1,0:T(8,128)S(1)} %broadcast_maximum_fusion, f32[2048]{0:T(1024)S(1)} %bitcast.31), kind=kLoop, calls=%fused_computation.3 | loop fusion | flops 16775168 | bytes 16801792 | tf_op jit(solution)/shard_map/reduce_sum | solution.py:53
  299.0 0.0 copy-start.3
  299.0 0.0 copy-start.4
  299.1 0.0 copy-start.5
  299.1 10.8 %fusion.15 = bf16[128,16,72]{0,2,1:T(8,128)(2,1)S(1)} fusion(bf16[2048,16,72]{0,2,1:T(8,128)(2,1)} %bitcast.27, f32[16,128,2048]{2,1,0:T(8,128)} %copy-done.1, f32[16,128]{1,0:T(8,128)S(1)} %broadcast_maximum_fusion, f32[2048]{0:T(1024)S(1)} %bitcast.32, f32[128,16]{0,1:T(8,128)S(1)} %bitcast.33), kind=kOutput, calls=%fused_computation.15 | convolution fusion | flops 621051904 | bytes 21815296 | tf_op jit(solution)/shard_map/hqk,khe->hqe/dot_general | solution.py:54
  309.9 0.6 fusion.28
  310.6 1.2 fusion.8
  (52 shorter events, 1.1 us)
Async XLA Ops:
  6.5 303.4 %copy-start = (bf16[1152,1152]{1,0:T(8,128)(2,1)S(1)}, bf16[1152,1152]{1,0:T(8,128)(2,1)}, u32[]{:S(2)}) copy-start(bf16[1152,1152]{1,0:T(8,128)(2,1)} %param.15) | copy-start | bytes 7962628
  6.5 271.8 %all-gather.4.cloned.1.call-start = ((), (), s32[]{:S(2)}) async-start(), calls=%async_computation | async-start | bytes 5013504 | tf_op jit(solution)/shard_map/all_gather | solution.py:89
  14.6 14.0 %collective-permute-start = (bf16[128,1152]{1,0:T(8,128)(2,1)S(1)}, bf16[128,1152]{1,0:T(8,128)(2,1)S(1)}, u32[]{:S(2)}, u32[]{:S(2)}) collective-permute-start(bf16[128,1152]{1,0:T(8,128)(2,1)S(1)} %slice.17), channel_id=1, source_target_pairs={{0,2},{2,4},{4,6},{6,8},{8,10},{10,12},{12,14},{14,16},{16,18},{18... | collective-permute-start | bytes 884744 | tf_op jit(solution)/shard_map/ppermute | solution.py:93
  28.6 11.8 %collective-permute-start.1 = (bf16[128,1152]{1,0:T(8,128)(2,1)S(1)}, bf16[128,1152]{1,0:T(8,128)(2,1)S(1)}, u32[]{:S(2)}, u32[]{:S(2)}) collective-permute-start(bf16[128,1152]{1,0:T(8,128)(2,1)S(1)} %collective-permute-done), channel_id=1, source_target_pairs={{0,2},{2,4},{4,6},{6,8},{8,10},{10,12},{12,14},{14,16},{16,18},{18... | collective-permute-start | bytes 884744 | tf_op jit(solution)/shard_map/ppermute | solution.py:93
  40.4 10.9 %collective-permute-start.2 = (bf16[128,1152]{1,0:T(8,128)(2,1)S(1)}, bf16[128,1152]{1,0:T(8,128)(2,1)S(1)}, u32[]{:S(2)}, u32[]{:S(2)}) collective-permute-start(bf16[128,1152]{1,0:T(8,128)(2,1)S(1)} %collective-permute-done.1), channel_id=1, source_target_pairs={{0,2},{2,4},{4,6},{6,8},{8,10},{10,12},{12,14},{14,16},{16,18},{18... | collective-permute-start | bytes 884744 | tf_op jit(solution)/shard_map/ppermute | solution.py:93
  51.3 10.3 %collective-permute-start.3 = (bf16[128,1152]{1,0:T(8,128)(2,1)S(1)}, bf16[128,1152]{1,0:T(8,128)(2,1)S(1)}, u32[]{:S(2)}, u32[]{:S(2)}) collective-permute-start(bf16[128,1152]{1,0:T(8,128)(2,1)S(1)} %collective-permute-done.2), channel_id=1, source_target_pairs={{0,2},{2,4},{4,6},{6,8},{8,10},{10,12},{12,14},{14,16},{16,18},{18... | collective-permute-start | bytes 884744 | tf_op jit(solution)/shard_map/ppermute | solution.py:93
  61.6 10.3 %collective-permute-start.4 = (bf16[128,1152]{1,0:T(8,128)(2,1)S(1)}, bf16[128,1152]{1,0:T(8,128)(2,1)S(1)}, u32[]{:S(2)}, u32[]{:S(2)}) collective-permute-start(bf16[128,1152]{1,0:T(8,128)(2,1)S(1)} %collective-permute-done.3), channel_id=1, source_target_pairs={{0,2},{2,4},{4,6},{6,8},{8,10},{10,12},{12,14},{14,16},{16,18},{18... | collective-permute-start | bytes 884744 | tf_op jit(solution)/shard_map/ppermute | solution.py:93
  71.9 10.3 %collective-permute-start.5 = (bf16[128,1152]{1,0:T(8,128)(2,1)S(1)}, bf16[128,1152]{1,0:T(8,128)(2,1)S(1)}, u32[]{:S(2)}, u32[]{:S(2)}) collective-permute-start(bf16[128,1152]{1,0:T(8,128)(2,1)S(1)} %collective-permute-done.4), channel_id=1, source_target_pairs={{0,2},{2,4},{4,6},{6,8},{8,10},{10,12},{12,14},{14,16},{16,18},{18... | collective-permute-start | bytes 884744 | tf_op jit(solution)/shard_map/ppermute | solution.py:93
  82.2 11.2 %collective-permute-start.6 = (bf16[128,1152]{1,0:T(8,128)(2,1)S(1)}, bf16[128,1152]{1,0:T(8,128)(2,1)S(1)}, u32[]{:S(2)}, u32[]{:S(2)}) collective-permute-start(bf16[128,1152]{1,0:T(8,128)(2,1)S(1)} %collective-permute-done.5), channel_id=1, source_target_pairs={{0,2},{2,4},{4,6},{6,8},{8,10},{10,12},{12,14},{14,16},{16,18},{18... | collective-permute-start | bytes 884744 | tf_op jit(solution)/shard_map/ppermute | solution.py:93
  93.4 12.3 %collective-permute-start.7 = (bf16[128,1152]{1,0:T(8,128)(2,1)S(1)}, bf16[128,1152]{1,0:T(8,128)(2,1)S(1)}, u32[]{:S(2)}, u32[]{:S(2)}) collective-permute-start(bf16[128,1152]{1,0:T(8,128)(2,1)S(1)} %collective-permute-done.6), channel_id=1, source_target_pairs={{0,2},{2,4},{4,6},{6,8},{8,10},{10,12},{12,14},{14,16},{16,18},{18... | collective-permute-start | bytes 884744 | tf_op jit(solution)/shard_map/ppermute | solution.py:93
  105.7 13.5 %collective-permute-start.8 = (bf16[128,1152]{1,0:T(8,128)(2,1)S(1)}, bf16[128,1152]{1,0:T(8,128)(2,1)S(1)}, u32[]{:S(2)}, u32[]{:S(2)}) collective-permute-start(bf16[128,1152]{1,0:T(8,128)(2,1)S(1)} %collective-permute-done.7), channel_id=1, source_target_pairs={{0,2},{2,4},{4,6},{6,8},{8,10},{10,12},{12,14},{14,16},{16,18},{18... | collective-permute-start | bytes 884744 | tf_op jit(solution)/shard_map/ppermute | solution.py:93
  119.2 12.6 %collective-permute-start.9 = (bf16[128,1152]{1,0:T(8,128)(2,1)S(1)}, bf16[128,1152]{1,0:T(8,128)(2,1)S(1)}, u32[]{:S(2)}, u32[]{:S(2)}) collective-permute-start(bf16[128,1152]{1,0:T(8,128)(2,1)S(1)} %collective-permute-done.8), channel_id=1, source_target_pairs={{0,2},{2,4},{4,6},{6,8},{8,10},{10,12},{12,14},{14,16},{16,18},{18... | collective-permute-start | bytes 884744 | tf_op jit(solution)/shard_map/ppermute | solution.py:93
  131.8 11.8 %collective-permute-start.10 = (bf16[128,1152]{1,0:T(8,128)(2,1)S(1)}, bf16[128,1152]{1,0:T(8,128)(2,1)S(1)}, u32[]{:S(2)}, u32[]{:S(2)}) collective-permute-start(bf16[128,1152]{1,0:T(8,128)(2,1)S(1)} %collective-permute-done.9), channel_id=1, source_target_pairs={{0,2},{2,4},{4,6},{6,8},{8,10},{10,12},{12,14},{14,16},{16,18},{18... | collective-permute-start | bytes 884744 | tf_op jit(solution)/shard_map/ppermute | solution.py:93
  143.6 10.9 %collective-permute-start.11 = (bf16[128,1152]{1,0:T(8,128)(2,1)S(1)}, bf16[128,1152]{1,0:T(8,128)(2,1)S(1)}, u32[]{:S(2)}, u32[]{:S(2)}) collective-permute-start(bf16[128,1152]{1,0:T(8,128)(2,1)S(1)} %collective-permute-done.10), channel_id=1, source_target_pairs={{0,2},{2,4},{4,6},{6,8},{8,10},{10,12},{12,14},{14,16},{16,18},{18... | collective-permute-start | bytes 884744 | tf_op jit(solution)/shard_map/ppermute | solution.py:93
  154.5 10.3 %collective-permute-start.12 = (bf16[128,1152]{1,0:T(8,128)(2,1)S(1)}, bf16[128,1152]{1,0:T(8,128)(2,1)S(1)}, u32[]{:S(2)}, u32[]{:S(2)}) collective-permute-start(bf16[128,1152]{1,0:T(8,128)(2,1)S(1)} %collective-permute-done.11), channel_id=1, source_target_pairs={{0,2},{2,4},{4,6},{6,8},{8,10},{10,12},{12,14},{14,16},{16,18},{18... | collective-permute-start | bytes 884744 | tf_op jit(solution)/shard_map/ppermute | solution.py:93
  164.8 10.3 %collective-permute-start.13 = (bf16[128,1152]{1,0:T(8,128)(2,1)S(1)}, bf16[128,1152]{1,0:T(8,128)(2,1)S(1)}, u32[]{:S(2)}, u32[]{:S(2)}) collective-permute-start(bf16[128,1152]{1,0:T(8,128)(2,1)S(1)} %collective-permute-done.12), channel_id=1, source_target_pairs={{0,2},{2,4},{4,6},{6,8},{8,10},{10,12},{12,14},{14,16},{16,18},{18... | collective-permute-start | bytes 884744 | tf_op jit(solution)/shard_map/ppermute | solution.py:93
  175.2 10.3 %collective-permute-start.14 = (bf16[128,1152]{1,0:T(8,128)(2,1)S(1)}, bf16[128,1152]{1,0:T(8,128)(2,1)S(1)}, u32[]{:S(2)}, u32[]{:S(2)}) collective-permute-start(bf16[128,1152]{1,0:T(8,128)(2,1)S(1)} %collective-permute-done.13), channel_id=1, source_target_pairs={{0,2},{2,4},{4,6},{6,8},{8,10},{10,12},{12,14},{14,16},{16,18},{18... | collective-permute-start | bytes 884744 | tf_op jit(solution)/shard_map/ppermute | solution.py:93
  187.5 3.6 %copy-start.2 = (bf16[4096,1152]{1,0:T(8,128)(2,1)}, bf16[4096,1152]{1,0:T(8,128)(2,1)S(1)}, u32[]{:S(2)}) copy-start(bf16[4096,1152]{1,0:T(8,128)(2,1)S(1)} %get-tuple-element.6) | copy-start | bytes 28311556
  289.5 5.7 %copy-start.1 = (f32[16,128,2048]{2,1,0:T(8,128)}, f32[16,128,2048]{2,1,0:T(8,128)S(1)}, u32[]{:S(2)}) copy-start(f32[16,128,2048]{2,1,0:T(8,128)S(1)} %get-tuple-element.13) | copy-start | bytes 50331652
  299.0 11.5 %copy-start.3 = (bf16[128,1152]{1,0:T(8,128)(2,1)S(1)}, bf16[128,1152]{1,0:T(8,128)(2,1)}, u32[]{:S(2)}) copy-start(bf16[128,1152]{1,0:T(8,128)(2,1)} %param.8) | copy-start | bytes 884740
  299.0 11.5 %copy-start.4 = (f32[1152]{0:T(1024)S(1)}, f32[1152]{0:T(1024)}, u32[]{:S(2)}) copy-start(f32[1152]{0:T(1024)} %param.13) | copy-start | bytes 13828
  299.1 11.5 %copy-start.5 = (s32[128]{0:T(128)S(1)}, s32[128]{0:T(128)}, u32[]{:S(2)}) copy-start(s32[128]{0:T(128)} %param.9) | copy-start | bytes 1540
Sparse Core Ops, SparseCore 0:
  191.3 75.6 all-gather.3
